TPU v7x, 256 devices: a 8x8x2 block of a 8x8x16 slice. The times are simulated.
256 devices in a mesh: groups: 2 (over z), ep: 128 (over y, x, core).
Axes of the slice: x: 8, y: 8, z: 2, core: 2. Of those that a mesh axis runs over, the one named last changes fastest.
The devices are a block of a 8x8x16 slice.
Arguments:
- tokens: bfloat16 [2048, 7168], P(('groups', 'ep')), parts along dimension 0, may hold values from -6 to 6
- experts: int32 [2048, 8], P(('groups', 'ep')), parts along dimension 0, may hold values from 0 to 15, as said below
- gate_fixed: int32 [2048, 8], P(('groups', 'ep')), parts along dimension 0, may hold values from 1 to 65535
- home_slot: int32 [2048], P(('groups', 'ep')), parts along dimension 0, may hold values from 0 to 7, as said below
- bias: float32 [16], replicated, may hold values from -0.5 to 0.5
- w_gate: bfloat16 [7168, 32768], P(None, 'ep'), may hold values from -0.0625 to 0.0625
- w_up: bfloat16 [7168, 32768], P(None, 'ep'), may hold values from -0.0625 to 0.0625
- w_down: bfloat16 [32768, 7168], P('ep'), may hold values from -0.125 to 0.125
Outputs:
- moe_out: bfloat16 [2048, 7168], P(('groups', 'ep')), parts along dimension 0
- bias_next: float32 [32], P('groups'), parts along dimension 0
There are 2 independent parts, one for each index of `groups`. A program takes and returns all parts, laid end to end along the dimension named above; an argument that names none is the same for every part. Nothing has to cross between parts.
Inputs may be any that keep to these rules, and one draw needn't show every extreme that they name: Each token names 8 different experts; among the tokens of one device no expert is named more than 6 times, and some device reaches that bound. `home_slot`: within each device's block of 8 tokens every value appears exactly once.
All inputs are finite; a program needn't handle non-finite values.
Results may differ from a plain program's by a relative error of at most 0.008.
Values may be sent and summed in bfloat16 or wider, within the bound.
A program may use at most 128 MiB of HBM per device.

v0:
```python
import math
import jax
import jax.numpy as jnp
from jax import lax
from jax.sharding import PartitionSpec as P

ROUTED_SCALE = 2.5


def per_device(tokens, experts, gate_fixed, home_slot, bias, w_gate, w_up, w_down):
    tok_rows, width = tokens.shape
    top_count = experts.shape[1]
    expert_count = bias.shape[0]
    device_count = lax.axis_size("ep")
    shards = device_count // expert_count
    meta = jnp.concatenate([experts, gate_fixed // 256, gate_fixed % 256], axis=1)
    rows = jnp.concatenate([tokens, meta.astype(jnp.bfloat16)], axis=1)
    placer = (home_slot[None, :] == jnp.arange(tok_rows, dtype=jnp.int32)[:, None]).astype(
        jnp.bfloat16
    )
    rows = jnp.dot(placer, rows, preferred_element_type=jnp.float32).astype(jnp.bfloat16)
    everyone = lax.all_gather(rows, "ep", axis=0, tiled=True)
    x = everyone[:, :width]
    meta = everyone[:, width:].astype(jnp.float32)
    ids, high, low = (
        meta[:, :top_count],
        meta[:, top_count : 2 * top_count],
        meta[:, 2 * top_count :],
    )
    fixed = high * 256.0 + low
    share = ROUTED_SCALE * fixed / jnp.sum(fixed, axis=1, keepdims=True)
    own = (lax.axis_index("ep") // shards).astype(jnp.float32)
    gate = jnp.sum(jnp.where(ids == own, share, 0.0), axis=1, keepdims=True)
    gate_part = jnp.dot(x, w_gate, preferred_element_type=jnp.float32)
    up_part = jnp.dot(x, w_up, preferred_element_type=jnp.float32)
    hidden = (jax.nn.silu(gate_part) * up_part * gate).astype(jnp.bfloat16)
    part = jnp.dot(hidden, w_down, preferred_element_type=jnp.float32).astype(jnp.bfloat16)
    out = lax.psum_scatter(part, "ep", scatter_dimension=0, tiled=True)
    hits = ids[:, :, None] == jnp.arange(expert_count, dtype=jnp.float32)[None, None, :]
    loads = jnp.sum(hits.astype(jnp.float32), axis=(0, 1))
    average = tok_rows * device_count * top_count / expert_count
    bias_next = bias + 2.0 / math.sqrt(average) * (average - loads)
    return (out, bias_next)


def solution(mesh):
    placed = (
        P(("groups", "ep"), None),
        P(("groups", "ep"), None),
        P(("groups", "ep"), None),
        P(("groups", "ep")),
        P(),
        P(None, "ep"),
        P(None, "ep"),
        P("ep", None),
    )
    return jax.shard_map(
        per_device,
        mesh=mesh,
        in_specs=placed,
        out_specs=(P(("groups", "ep"), None), P("groups")),
        check_vma=False,
    )
```

profile of v0, /device:TPU:516, one launch (start us, length us, event | category | flops | bytes accessed | tf_op | source)
XLA Modules:
  0.0 376.1 jit_solution(18024475353310165763)
XLA Ops:
  7.2 0.1 all-gather.2.cloned.1.call-start
  7.2 0.7 convert.9
  7.9 0.7 fusion.24
  8.6 1.0 concatenate.6
  9.6 1.5 convolution_convert_fusion.1
  11.1 0.1 all-gather.2.cloned.1.call-update
  11.1 0.1 reduce-scatter.2.cloned.1.call-start
  11.2 110.1 %all-gather.2.cloned.1.call-done = bf16[1024,7192]{1,0:T(8,128)(2,1)} async-done(((bf16[8,7192]{1,0:T(8,128)(2,1)}), bf16[1024,7192]{1,0:T(8,128)(2,1)}) %all-gather.2.cloned.1.call-update) | async-done | bytes 14729232 | tf_op jit(solution)/shard_map/all_gather | solution.py:22
  121.3 1.0 slice_convert_fusion
  122.3 0.5 fusion.29
  122.8 0.6 select_reduce_fusion
  123.5 8.3 %fusion.2 = f32[1024,256]{1,0:T(8,128)S(1)} fusion(bf16[7168,256]{1,0:T(8,128)(2,1)} %param.13, bf16[1024,7192]{1,0:T(8,128)(2,1)} %all-gather.2.cloned.1.call-done), kind=kOutput, calls=%fused_computation.3 | convolution fusion | flops 3758096384 | bytes 19398656 | tf_op jit(solution)/shard_map/dot_general | solution.py:34
  131.8 23.7 %convolution_convert_fusion = bf16[1024,7168]{1,0:T(8,128)(2,1)} fusion(bf16[256,7168]{1,0:T(8,128)(2,1)} %param.15, bf16[7168,256]{1,0:T(8,128)(2,1)} %param.14, bf16[1024,7192]{1,0:T(8,128)(2,1)} %all-gather.2.cloned.1.call-done, f32[1024,256]{1,0:T(8,128)S(1)} %fusion.2, f32[1024]{0:T(1024)S(1)} %select_reduce_fusion), kind=kOutput, calls=%fused_computation | convolution fusion | flops 7525367808 | bytes 37752832 | tf_op jit(solution)/shard_map/dot_general | solution.py:37
  155.5 0.0 copy-start
  155.5 0.1 reduce-scatter.2.cloned.1.call-update
  155.5 0.2 copy.10
  155.7 0.2 convert_reduce_fusion
  155.9 0.2 copy-done
  156.1 0.5 multiply_add_fusion
  156.6 212.6 %reduce-scatter.2.cloned.1.call-done = bf16[8,7168]{1,0:T(8,128)(2,1)} async-done(((bf16[1024,7168]{1,0:T(8,128)(2,1)}), bf16[8,7168]{1,0:T(8,128)(2,1)}) %reduce-scatter.2.cloned.1.call-update) | async-done | bytes 114704 | tf_op jit(solution)/shard_map/reduce_scatter | solution.py:38
Async XLA Ops:
  7.2 114.2 %all-gather.2.cloned.1.call-start = ((), (), s32[]{:S(2)}) async-start(), calls=%async_computation.1 | async-start | bytes 15058944 | tf_op jit(solution)/shard_map/all_gather | solution.py:22
  11.1 358.1 %reduce-scatter.2.cloned.1.call-start = ((), (), s32[]{:S(2)}) async-start(), calls=%async_computation.2 | async-start | bytes 14794752 | tf_op jit(solution)/shard_map/reduce_scatter | solution.py:38
  155.5 0.7 copy-start
Sparse Core Ops, SparseCore 0:
  11.3 110.0 all-gather.1
  155.6 213.5 reduce-scatter.1
where the time goes:
time: 376 us
  waiting for transfers between devices  323 us (86%)
  matrix products  33.4 us (9%)
  between operations  14.1 us (4%)
  other arithmetic  4.24 us (1%)
    reduce_scatter x1, waiting for transfers between devices, per_device(): out = lax.psum_scatter(part, 'ep', scatter_dimension=0, tiled=True)  213 us
    all_gather x1, waiting for transfers between devices, per_device(): everyone = lax.all_gather(rows, 'ep', axis=0, tiled=True)  110 us
    dot_general x1, matrix products, per_device(): jnp.dot(hidden, w_down, preferred_element_type=jnp.float32)  23.7 us
    dot_general x1, matrix products, per_device(): gate_part = jnp.dot(x, w_gate, preferred_element_type=jnp.float32)  8.3 us
  transfers between devices with their start and end apart: 2, of which 2 were waited for; matrix products, arithmetic and copies ran while one was open for 0% of the time, Pallas kernels for 0%

commit v1 on v0

--- a/solution.py
+++ b/solution.py
@@ -19,7 +19,8 @@
         jnp.bfloat16
     )
     rows = jnp.dot(placer, rows, preferred_element_type=jnp.float32).astype(jnp.bfloat16)
-    everyone = lax.all_gather(rows, "ep", axis=0, tiled=True)
+    sent = jnp.stack([rows] * lax.axis_size("ep"))
+    everyone = jnp.concatenate(lax.all_to_all(sent, "ep", 0, 0), axis=0)
     x = everyone[:, :width]
     meta = everyone[:, width:].astype(jnp.float32)
     ids, high, low = (

time: 376 us -> 779 us (2.07)
  waiting for transfers between devices: 323 us -> 693 us
  starting transfers between devices: 0.13 us -> 27.5 us
    all_to_all x0 -> x1, waiting for transfers between devices: none -> 474 us  [per_device(): everyone = jnp.concatenate(lax.all_to_all(sent, 'ep', 0, 0), axis=0)]
    all_gather x1 -> x0, waiting for transfers between devices: 110 us -> none  [per_device(): everyone = lax.all_gather(rows, 'ep', axis=0, tiled=True)]
    all_to_all x0 -> x1, starting transfers between devices: none -> 27.2 us  [per_device(): everyone = jnp.concatenate(lax.all_to_all(sent, 'ep', 0, 0), axis=0)]
where the time goes in v1:
time: 779 us; the launch traced here: 778 us
  waiting for transfers between devices  693 us (89%)
  matrix products  32.8 us (4%)
  starting transfers between devices  27.5 us (4%)
  between operations  14.1 us (2%)
  local copies, waits for them, and re-layouts  8.64 us (1%)
    all_to_all x1, waiting for transfers between devices, per_device(): everyone = jnp.concatenate(lax.all_to_all(sent, 'ep', 0, 0), axis=0)  474 us
    reduce_scatter x1, waiting for transfers between devices, per_device(): out = lax.psum_scatter(part, 'ep', scatter_dimension=0, tiled=True)  219 us
    all_to_all x1, starting transfers between devices, per_device(): everyone = jnp.concatenate(lax.all_to_all(sent, 'ep', 0, 0), axis=0)  27.2 us
    dot_general x1, matrix products, per_device(): jnp.dot(hidden, w_down, preferred_element_type=jnp.float32)  23.7 us
  transfers between devices with their start and end apart: 2, of which 2 were waited for; matrix products, arithmetic and copies ran while one was open for 0% of the time, Pallas kernels for 0%

profile of v1, /device:TPU:516, one launch (start us, length us, event | category | flops | bytes accessed | tf_op | source)
XLA Modules:
  0.0 778.3 jit_solution(13545535758666934282)
XLA Ops:
  7.2 0.7 convert.9
  7.9 0.7 fusion.24
  8.6 1.0 concatenate.6
  9.6 0.8 convolution_convert_fusion.1
  10.4 6.2 stack.2
  16.6 27.2 %all-to-all-start = ((bf16[128,8,7192]{2,1,0:T(8,128)(2,1)}), bf16[128,8,7192]{2,1,0:T(8,128)(2,1)}, u32[]{:S(2)}, u32[]{:S(2)}) async-start(bf16[128,8,7192]{2,1,0:T(8,128)(2,1)} %stack.2), calls=%async_computation | async-start | bytes 29884416 | tf_op jit(solution)/shard_map/all_to_all | solution.py:23
  43.8 0.2 reduce-scatter.2.cloned.1.call-start
  44.0 473.7 %all-to-all-done = bf16[128,8,7192]{2,1,0:T(8,128)(2,1)} async-done(((bf16[128,8,7192]{2,1,0:T(8,128)(2,1)}), bf16[128,8,7192]{2,1,0:T(8,128)(2,1)}, u32[]{:S(2)}, u32[]{:S(2)}) %all-to-all-start) | async-done | bytes 14729248 | tf_op jit(solution)/shard_map/all_to_all | solution.py:23
  517.8 1.0 slice.21
  518.7 0.1 copy.20
  518.9 8.3 %fusion.2 = f32[1024,256]{1,0:T(8,128)S(1)} fusion(bf16[7168,256]{1,0:T(8,128)(2,1)} %param.13, bf16[1024,7192]{1,0:T(8,128)(2,1)} %bitcast), kind=kOutput, calls=%fused_computation.3 | convolution fusion | flops 3758096384 | bytes 19398656 | tf_op jit(solution)/shard_map/dot_general | solution.py:35
  527.2 23.7 %convolution_convert_fusion = bf16[1024,7168]{1,0:T(8,128)(2,1)} fusion(bf16[256,7168]{1,0:T(8,128)(2,1)} %param.15, bf16[7168,256]{1,0:T(8,128)(2,1)} %param.14, bf16[1024,7192]{1,0:T(8,128)(2,1)} %bitcast, f32[1024,256]{1,0:T(8,128)S(1)} %fusion.2, f32[1024]{0:T(1024)S(1)} %select_reduce_fusion), kind=kOutput, calls=%fused_computation | convolution fusion | flops 7525367808 | bytes 37752832 | tf_op jit(solution)/shard_map/dot_general | solution.py:38
  550.9 0.0 copy-start
  550.9 0.1 reduce-scatter.2.cloned.1.call-update
  551.0 0.2 convert_reduce_fusion
  551.2 0.4 copy-done
  551.5 0.5 multiply_add_fusion
  552.1 219.4 %reduce-scatter.2.cloned.1.call-done = bf16[8,7168]{1,0:T(8,128)(2,1)} async-done(((bf16[1024,7168]{1,0:T(8,128)(2,1)}), bf16[8,7168]{1,0:T(8,128)(2,1)}) %reduce-scatter.2.cloned.1.call-update) | async-done | bytes 114704 | tf_op jit(solution)/shard_map/reduce_scatter | solution.py:39
  (4 shorter events, 0.1 us)
Async XLA Ops:
  16.6 501.2 %all-to-all-start = ((bf16[128,8,7192]{2,1,0:T(8,128)(2,1)}), bf16[128,8,7192]{2,1,0:T(8,128)(2,1)}, u32[]{:S(2)}, u32[]{:S(2)}) async-start(bf16[128,8,7192]{2,1,0:T(8,128)(2,1)} %stack.2), calls=%async_computation | async-start | bytes 29884416 | tf_op jit(solution)/shard_map/all_to_all | solution.py:23
  43.8 727.7 %reduce-scatter.2.cloned.1.call-start = ((), (), s32[]{:S(2)}) async-start(), calls=%async_computation.2 | async-start | bytes 14794752 | tf_op jit(solution)/shard_map/reduce_scatter | solution.py:39
  550.9 0.7 copy-start
Sparse Core Ops, SparseCore 0:
  551.1 220.3 reduce-scatter.1
